TPU v7x, 32 devices: a whole 2x2x4 slice. The times are simulated.
32 devices in a mesh: dp: 4 (over x, core), mp: 8 (over z, y).
Axes of the slice: x: 2, y: 2, z: 4, core: 2. Of those that a mesh axis runs over, the one named last changes fastest.
Arguments:
- attn_out: bfloat16 [512, 8192], P('dp', 'mp'), may hold values from -6 to 6
- residual: bfloat16 [512, 8192], P('dp', 'mp'), may hold values from -40 to 40
- output_weight: bfloat16 [8192, 8192], P('mp', 'dp'), may hold values from -0.0625 to 0.0625
- prune_mask: int32 [8192, 128], P('mp'), may hold values 0 or 1
- inverse_factor: float32 [128, 8192], P(None, 'dp'), may hold values from -2 to 2, as said below
- norm_gain: bfloat16 [8192], P('mp'), may hold values from 0.5 to 1.5
- gate_up_weight: bfloat16 [8192, 2, 14336], P('dp', None, 'mp'), may hold values from -0.0625 to 0.0625
Outputs:
- pruned_weight: bfloat16 [8192, 8192], P('mp', 'dp')
- stream: bfloat16 [512, 8192], P('dp', 'mp')
- hessian: float32 [14336, 14336], P('mp', 'dp')
Inputs may be any that keep to these rules, and one draw needn't show every extreme that they name: inverse_factor is zero below its diagonal, and its diagonal lies between 0.5 and 2.
All inputs are finite; a program needn't handle non-finite values. No bound on the sum of `prune_mask` on one device may be relied on, other than what follows from the above.
Results may differ from a plain program's by a relative error of at most 0.012.
Values may be sent and summed in bfloat16 or wider, within the bound.
A program may use at most 128 MiB of HBM per device.

v0:
```python
import jax
import jax.numpy as jnp
from jax import lax
from jax.sharding import PartitionSpec as P


def from_root(block, axis, holder):
    block = jnp.where(lax.axis_index(axis) == holder, block, jnp.zeros_like(block))
    return lax.psum(block, axis)


def body(attn_out, residual, output_weight, prune_mask, inverse_factor, norm_gain, gate_up_weight):
    width_block = prune_mask.shape[1]
    kept_mask = prune_mask.astype(jnp.float32)
    weight_cols = output_weight.astype(jnp.float32)
    is_first = lax.axis_index("dp") == 0
    factor_block = inverse_factor[:, :width_block]
    pivots = jnp.where(is_first, jnp.diagonal(factor_block), 1.0)
    cutting = (1.0 - kept_mask) / pivots[None, :]
    sub_width = min(32, width_block)
    strict = jnp.tril(jnp.ones((sub_width, sub_width), jnp.float32), -1)
    identity_sub = jnp.eye(sub_width, dtype=jnp.float32)[None, :, :]
    pieces = []
    for begin in range(0, width_block, sub_width):
        current = weight_cols[:, begin : begin + sub_width]
        if begin > 0:
            earlier = jnp.concatenate(pieces, axis=1)
            current = current - jnp.dot(
                earlier,
                factor_block[:begin, begin : begin + sub_width],
                precision=lax.Precision.HIGHEST,
                preferred_element_type=jnp.float32,
            )
        cut_part = cutting[:, begin : begin + sub_width]
        inner = factor_block[begin : begin + sub_width, begin : begin + sub_width]
        system = cut_part[:, :, None] * (inner.T * strict)[None, :, :] + identity_sub
        target = (cut_part * current)[:, :, None]
        pieces.append(
            jax.scipy.linalg.solve_triangular(system, target, lower=True, unit_diagonal=True)[
                :, :, 0
            ]
        )
    solved = jnp.concatenate(pieces, axis=1)
    errors = from_root(solved, "dp", 0)
    updated = weight_cols - jnp.dot(
        errors, inverse_factor, precision=lax.Precision.HIGHEST, preferred_element_type=jnp.float32
    )
    leading = jnp.where(is_first, updated[:, :width_block] * kept_mask, updated[:, :width_block])
    pruned_weight = lax.dynamic_update_slice_in_dim(updated, leading, 0, 1).astype(jnp.bfloat16)
    features = lax.all_gather(attn_out, "mp", axis=1, tiled=True)
    projected = lax.dot_general(
        features,
        lax.all_gather(pruned_weight, "dp", axis=1, tiled=True),
        (((1,), (1,)), ((), ())),
        preferred_element_type=jnp.float32,
    )
    stream = (residual.astype(jnp.float32) + projected).astype(jnp.bfloat16)
    width_model = features.shape[1]
    stream_float = stream.astype(jnp.float32)
    squares = lax.psum(jnp.sum(stream_float * stream_float, axis=1), "mp")
    inverse = lax.rsqrt(squares / width_model + 1e-05)
    normed = (stream_float * inverse[:, None] * norm_gain.astype(jnp.float32)[None, :]).astype(
        jnp.bfloat16
    )
    normed_all = lax.all_gather(normed, "mp", axis=1, tiled=True)
    input_rows = gate_up_weight.shape[0]
    unit_count = gate_up_weight.shape[2]
    slices = lax.all_to_all(normed_all, "dp", split_axis=1, concat_axis=0, tiled=True)
    flat_weight = gate_up_weight.reshape(input_rows, 2 * unit_count)
    gate_up = lax.psum_scatter(
        jnp.dot(slices, flat_weight, preferred_element_type=jnp.float32),
        "dp",
        scatter_dimension=0,
        tiled=True,
    )
    gate_part = gate_up[:, :unit_count]
    up_part = gate_up[:, unit_count:]
    hidden = (jax.nn.silu(gate_part) * up_part).astype(jnp.bfloat16)
    hidden_all = lax.all_gather(hidden, "mp", axis=1, tiled=True)
    count_rows = hidden_all.shape[1] // lax.axis_size("mp")
    window_local = lax.dynamic_slice_in_dim(
        hidden_all, lax.axis_index("mp") * count_rows, count_rows, 1
    )
    weighting = 2.0 / (hidden_all.shape[0] * lax.axis_size("dp"))
    contract = (((0,), (0,)), ((), ()))
    columns = lax.all_to_all(hidden_all, "dp", split_axis=1, concat_axis=0, tiled=True)
    window_all = lax.all_gather(window_local, "dp", axis=0, tiled=True)
    hessian = weighting * lax.dot_general(
        window_all, columns, contract, preferred_element_type=jnp.float32
    )
    return (pruned_weight, stream, hessian)


def solution(mesh):
    in_specs = (
        P("dp", "mp"),
        P("dp", "mp"),
        P("mp", "dp"),
        P("mp", None),
        P(None, "dp"),
        P("mp"),
        P("dp", None, "mp"),
    )
    out_specs = (P("mp", "dp"), P("dp", "mp"), P("mp", "dp"))
    return jax.shard_map(body, mesh=mesh, in_specs=in_specs, out_specs=out_specs, check_vma=False)
```

profile of v0, /device:TPU:0, one launch (start us, length us, event | category | flops | bytes accessed | tf_op | source)
XLA Modules:
  0.0 952.4 jit_solution(11305181622557403256)
XLA Ops:
  8.0 0.0 all-reduce.2.cloned.1.call-start
  8.1 0.9 select_multiply_fusion.3
  8.9 0.1 iota_compare_fusion.1
  9.0 1.2 copy.21
  10.3 6.4 copy.20
  16.7 6.7 convert_element_type.40
  23.3 0.1 copy.22
  23.4 0.1 copy.23
  23.5 0.1 copy.24
  23.5 0.1 copy.25
  23.6 1.3 gather_fusion
  24.9 0.1 subtract_divide_fusion
  25.0 1.0 slice_multiply_fusion.1
  26.0 7.3 add_bitcast_fusion.3
  33.3 100.7 %custom-call.8 = f32[1024,1,32,32]{0,2,3,1:T(8,128)} custom-call(f32[1024,1,32,32]{0,3,2,1:T(8,128)} %get-tuple-element.19), custom_call_target="InvertDiagBlocksLowerTriangular" | custom-call | tf_op jit(solution)/shard_map/jit(_solve_triangular)/vmap()/triangular_solve | solution.py:39
  134.0 2.7 fusion.3
  136.7 1.3 fusion.7
  138.0 100.7 %custom-call.9 = f32[1024,1,32,32]{0,2,3,1:T(8,128)} custom-call(f32[1024,1,32,32]{0,3,2,1:T(8,128)} %get-tuple-element.20), custom_call_target="InvertDiagBlocksLowerTriangular" | custom-call | tf_op jit(solution)/shard_map/jit(_solve_triangular)/vmap()/triangular_solve | solution.py:39
  238.7 2.7 fusion.2
  241.4 1.3 fusion.8
  242.7 100.6 %custom-call.10 = f32[1024,1,32,32]{0,2,3,1:T(8,128)} custom-call(f32[1024,1,32,32]{0,3,2,1:T(8,128)} %get-tuple-element.21), custom_call_target="InvertDiagBlocksLowerTriangular" | custom-call | tf_op jit(solution)/shard_map/jit(_solve_triangular)/vmap()/triangular_solve | solution.py:39
  343.3 2.7 fusion.1
  346.0 1.3 fusion.6
  347.4 100.6 %custom-call.11 = f32[1024,1,32,32]{0,2,3,1:T(8,128)} custom-call(f32[1024,1,32,32]{0,3,2,1:T(8,128)} %get-tuple-element.22), custom_call_target="InvertDiagBlocksLowerTriangular" | custom-call | tf_op jit(solution)/shard_map/jit(_solve_triangular)/vmap()/triangular_solve | solution.py:39
  448.0 2.7 fusion
  450.7 0.8 maximum_select_fusion
  451.5 0.0 all-reduce.2.cloned.1.call-update
  451.5 0.0 all-gather.8.cloned.1.call-start
  451.6 0.5 all-gather.8.cloned.1.call-update
  452.1 0.2 all-gather.6.cloned.1.call-start
  452.4 35.5 %all-reduce.2.cloned.1.call-done = f32[1024,128]{0,1:T(8,128)} async-done(((f32[1024,128]{0,1:T(8,128)}), f32[1024,128]{0,1:T(8,128)}) %all-reduce.2.cloned.1.call-update) | async-done | bytes 524304 | tf_op jit(solution)/shard_map/psum | solution.py:9
  487.8 12.2 %convolution_subtract_fusion = f32[1024,2048]{0,1:T(8,128)S(1)} fusion(f32[1024,128]{0,1:T(8,128)} %all-reduce.2.cloned.1.call-done, f32[128,2048]{1,0:T(8,128)S(1)} %copy-done, bf16[1024,2048]{0,1:T(8,128)(2,1)} %copy.20), kind=kOutput, calls=%fused_computation.2 | convolution fusion | flops 3225419776 | bytes 14155776 | tf_op jit(solution)/shard_map/dot_general | solution.py:45
  500.0 0.2 fusion.13
  500.2 2.6 convert_element_type.43
  502.8 0.0 all-gather.6.cloned.1.call-update
  502.9 0.0 all-gather.10.cloned.1.call-start
  502.9 0.9 copy-done.1
  503.8 0.2 copy.27
  504.0 1.9 all-gather.8.cloned.1.call-done
  505.9 105.8 %all-gather.6.cloned.1.call-done = bf16[1024,8192]{0,1:T(8,128)(2,1)} async-done(((bf16[1024,2048]{0,1:T(8,128)(2,1)}), bf16[1024,8192]{0,1:T(8,128)(2,1)}) %all-gather.6.cloned.1.call-update) | async-done | bytes 16777232 | tf_op jit(solution)/shard_map/all_gather | solution.py:53
  611.7 10.9 %fusion.10 = (f32[128]{0:T(128)S(1)}, bf16[128,1024]{0,1:T(8,128)(2,1)S(1)}) fusion(bf16[1024,8192]{0,1:T(8,128)(2,1)} %all-gather.6.cloned.1.call-done, bf16[128,8192]{1,0:T(8,128)(2,1)} %all-gather.8.cloned.1.call-done, bf16[128,1024]{0,1:T(8,128)(2,1)S(1)} %copy.27), kind=kOutput, calls=%fused_computation.30 | convolution fusion | flops 2148270080 | bytes 19399168 | tf_op jit(solution)/shard_map/dot_general | solution.py:51
  622.7 21.4 %psum.15 = f32[128]{0:T(128)S(1)} all-reduce(f32[128]{0:T(128)S(1)} %get-tuple-element.23), channel_id=1, replica_groups=mesh['dp'=4,'mp'=8] {'mp'}, use_global_device_ids=true, to_apply=%region_2.4 | all-reduce | flops 128 | bytes 1024 | tf_op jit(solution)/shard_map/psum | solution.py:60
  644.0 0.9 fusion.12
  645.0 0.0 all-gather.10.cloned.1.call-update
  645.0 45.4 %all-gather.10.cloned.1.call-done = bf16[128,8192]{0,1:T(8,128)(2,1)} async-done(((bf16[128,1024]{0,1:T(8,128)(2,1)}), bf16[128,8192]{0,1:T(8,128)(2,1)}) %all-gather.10.cloned.1.call-update) | async-done | bytes 2097168 | tf_op jit(solution)/shard_map/all_gather | solution.py:65
  690.4 3.9 copy.28
  694.3 3.6 all-to-all-start
  697.9 0.3 reduce-scatter.2.cloned.1.call-start
  698.2 16.0 %copy.58 = bf16[256,8,2,1792]{3,1,2,0:T(8,128)(2,1)} copy(bf16[256,8,2,1792]{3,2,1,0:T(2,128)(2,1)} %bitcast.78) | data formatting | bytes 29360128
  714.2 9.3 all-to-all-done
  723.6 12.9 %fusion.29 = f32[512,3584]{1,0:T(8,128)} fusion(bf16[512,2048]{1,0:T(8,128)(2,1)S(1)} %bitcast.82, bf16[2048,3584]{1,0:T(8,128)(2,1)} %bitcast.79), kind=kOutput, calls=%fused_computation.65 | convolution fusion | flops 7516192768 | bytes 24117248 | tf_op jit(solution)/shard_map/dot_general | solution.py:71
  736.5 0.0 all-gather.12.cloned.1.call-start
  736.5 63.7 %reduce-scatter.2.cloned.1.call-done = f32[128,3584]{1,0:T(8,128)} async-done(((f32[512,3584]{1,0:T(8,128)}), f32[128,3584]{1,0:T(8,128)}) %reduce-scatter.2.cloned.1.call-update) | async-done | bytes 1835024 | tf_op jit(solution)/shard_map/reduce_scatter | solution.py:70
  800.3 2.5 fusion.9
  802.7 0.0 all-gather.12.cloned.1.call-update
  802.8 66.2 %all-gather.12.cloned.1.call-done = bf16[128,14336]{1,0:T(8,128)(2,1)} async-done(((bf16[128,1792]{1,0:T(8,128)(2,1)}), bf16[128,14336]{1,0:T(8,128)(2,1)}) %all-gather.12.cloned.1.call-update) | async-done | bytes 3670032 | tf_op jit(solution)/shard_map/all_gather | solution.py:79
  869.0 4.2 copy.60
  873.2 4.7 all-to-all-start.1
  877.9 0.0 all-gather.14.cloned.1.call-start
  878.0 1.8 constant_dynamic-slice_fusion
  879.8 6.4 copy.30
  886.2 0.8 copy.31
  887.1 43.2 %all-to-all-done.1 = bf16[128,4,3584]{2,0,1:T(8,128)(2,1)} async-done(((bf16[128,4,3584]{2,0,1:T(8,128)(2,1)}), bf16[128,4,3584]{2,0,1:T(8,128)(2,1)}, u32[]{:S(2)}, u32[]{:S(2)}) %all-to-all-start.1) | async-done | bytes 3670048 | tf_op jit(solution)/shard_map/all_to_all | solution.py:86
  930.3 14.7 %convolution_multiply_fusion = f32[1792,3584]{1,0:T(8,128)} fusion(bf16[512,1792]{1,0:T(8,128)(2,1)} %all-gather.14.cloned.1.call-done, bf16[512,3584]{1,0:T(8,128)(2,1)} %bitcast.34), kind=kOutput, calls=%fused_computation.1 | convolution fusion | flops 6583091200 | bytes 31195136 | tf_op jit(solution)/shard_map/dot_general | solution.py:88
  (16 shorter events, 0.1 us)
Async XLA Ops:
  8.0 479.9 %all-reduce.2.cloned.1.call-start = ((), (), s32[]{:S(2)}) async-start(), calls=%async_computation.3 | async-start | bytes 1048576 | tf_op jit(solution)/shard_map/psum | solution.py:9
  16.7 7.0 slice-start
  33.2 103.4 %copy-start = (f32[128,2048]{1,0:T(8,128)S(1)}, f32[128,2048]{1,0:T(8,128)}, u32[]{:S(2)}) copy-start(f32[128,2048]{1,0:T(8,128)} %param.13) | copy-start | bytes 3145732
  451.5 54.4 %all-gather.8.cloned.1.call-start = ((), (), s32[]{:S(2)}) async-start(), calls=%async_computation.5 | async-start | bytes 2359296 | tf_op jit(solution)/shard_map/all_gather | solution.py:50
  452.1 159.6 %all-gather.6.cloned.1.call-start = ((), (), s32[]{:S(2)}) async-start(), calls=%async_computation.4 | async-start | bytes 20971520 | tf_op jit(solution)/shard_map/all_gather | solution.py:53
  502.8 0.9 copy-start.1
  502.8 1.1 copy-start.2
  502.9 187.5 %all-gather.10.cloned.1.call-start = ((), (), s32[]{:S(2)}) async-start(), calls=%async_computation.6 | async-start | bytes 2359296 | tf_op jit(solution)/shard_map/all_gather | solution.py:65
  694.3 29.2 %all-to-all-start = ((bf16[128,4,2048]{2,0,1:T(8,128)(2,1)}), bf16[128,4,2048]{2,0,1:T(8,128)(2,1)S(1)}, u32[]{:S(2)}, u32[]{:S(2)}) async-start(bf16[128,4,2048]{2,0,1:T(8,128)(2,1)} %copy.28), calls=%async_computation | async-start | bytes 4194304 | tf_op jit(solution)/shard_map/all_to_all | solution.py:68
  697.9 102.3 %reduce-scatter.2.cloned.1.call-start = ((), (), s32[]{:S(2)}) async-start(), calls=%async_computation.7 | async-start | bytes 9175040 | tf_op jit(solution)/shard_map/reduce_scatter | solution.py:70
  736.5 132.5 %all-gather.12.cloned.1.call-start = ((), (), s32[]{:S(2)}) async-start(), calls=%async_computation.8 | async-start | bytes 4128768 | tf_op jit(solution)/shard_map/all_gather | solution.py:79
  873.2 57.2 %all-to-all-start.1 = ((bf16[128,4,3584]{2,0,1:T(8,128)(2,1)}), bf16[128,4,3584]{2,0,1:T(8,128)(2,1)}, u32[]{:S(2)}, u32[]{:S(2)}) async-start(bf16[128,4,3584]{2,0,1:T(8,128)(2,1)} %bitcast.80), calls=%async_computation.2 | async-start | bytes 7340032 | tf_op jit(solution)/shard_map/all_to_all | solution.py:86
  877.9 52.4 %all-gather.14.cloned.1.call-start = ((), (), s32[]{:S(2)}) async-start(), calls=%async_computation.9 | async-start | bytes 2293760 | tf_op jit(solution)/shard_map/all_gather | solution.py:87
Sparse Core Ops, SparseCore 0:
  451.7 36.1 all-reduce.1
  736.6 63.6 reduce-scatter.1
  880.3 30.1 all-gather.13
Sparse Core Ops, SparseCore 1:
  454.2 51.6 all-gather.7
  507.3 104.3 all-gather.5
  645.1 45.3 all-gather.9
  802.9 66.1 all-gather.11
where the time goes:
time: 954 us; the launch traced here: 952 us
  other arithmetic  437 us (46%)
  waiting for transfers between devices  372 us (39%)
  matrix products  54.6 us (6%)
  local copies, waits for them, and re-layouts  43.5 us (5%)
  blocking collectives  21.4 us (2%)
  between operations  15.6 us (2%)
    another operation x12, other arithmetic, body(): jax.scipy.linalg.solve_triangular(system, target, lower=True, unit_diagon...  421 us
    all_gather x1, waiting for transfers between devices, body(): lax.all_gather(pruned_weight, 'dp', axis=1, tiled=True)  106 us
    all_gather x1, waiting for transfers between devices, body(): hidden_all = lax.all_gather(hidden, 'mp', axis=1, tiled=True)  66.2 us
    reduce_scatter x1, waiting for transfers between devices, body(): lax.psum_scatter(jnp.dot(slices, flat_weight, preferred_element_type=jnp....  63.7 us
    all_gather x1, waiting for transfers between devices, body(): normed_all = lax.all_gather(normed, 'mp', axis=1, tiled=True)  45.4 us
    all_to_all x1, waiting for transfers between devices, body(): lax.all_to_all(hidden_all, 'dp', split_axis=1, concat_axis=0, tiled=True)  43.2 us
    psum x1, waiting for transfers between devices, from_root(): return lax.psum(block, axis)  35.5 us
    unnamed x12, local copies, waits for them, and re-layouts  32 us
  transfers between devices with their start and end apart: 9, of which 8 were waited for; matrix products, arithmetic and copies ran while one was open for 4% of the time, Pallas kernels for 0%

commit v1 on v0

v1 whole, which is shorter than its diff:
```python
import functools

import jax
import jax.numpy as jnp
from jax import lax
from jax.experimental import pallas as pl
from jax.experimental.pallas import tpu as pltpu
from jax.sharding import PartitionSpec as P

GROUP = 8


def from_first(block, axis):
    size, index = lax.axis_size(axis), lax.axis_index(axis)
    stride = size // 2
    while stride >= 1:
        pairs = [(i, i + stride) for i in range(0, size, 2 * stride)]
        arrived = lax.ppermute(block, axis, pairs)
        block = jnp.where(index % (2 * stride) == stride, arrived, block)
        stride //= 2
    return block


def scatter_sum(partial, axis):
    size, index = lax.axis_size(axis), lax.axis_index(axis)
    rows, cols = partial.shape
    blocks = partial.reshape(size, rows // size, cols)
    stride, left = 1, size
    while left > 1:
        halves = blocks.reshape(left // 2, 2, rows // size, cols)
        bit = (index // stride) % 2
        keep = lax.dynamic_index_in_dim(halves, bit, 1, keepdims=False)
        give = lax.dynamic_index_in_dim(halves, 1 - bit, 1, keepdims=False)
        pairs = [(i, i ^ stride) for i in range(size)]
        arrived = lax.ppermute(give.astype(jnp.bfloat16), axis, pairs)
        blocks = keep + arrived.astype(jnp.float32)
        left //= 2
        stride *= 2
    return blocks[0]


def exchange(rows_block, axis):
    size = lax.axis_size(axis)
    rows, cols = rows_block.shape
    blocks = rows_block.reshape(rows, size, cols // size).transpose(1, 0, 2)
    swapped = lax.all_to_all(blocks, axis, split_axis=0, concat_axis=0, tiled=True)
    return swapped.reshape(size * rows, cols // size)


def solve_kernel(factor_ref, weight_ref, cutting_ref, error_ref):
    count = weight_ref.shape[0] // GROUP
    error_ref[...] = weight_ref[...]

    def step(block, carry):
        base = block * GROUP
        solved = []
        for i in range(GROUP):
            value = error_ref[base + i]
            for k in range(i):
                value = value - factor_ref[base + k, base + i] * solved[k]
            solved.append(value * cutting_ref[base + i])
        for i in range(GROUP):
            error_ref[base + i] = solved[i]

        def later(other, inner):
            place = other * GROUP
            for t in range(GROUP):
                value = error_ref[place + t]
                for k in range(GROUP):
                    value = value - factor_ref[base + k, place + t] * solved[k]
                error_ref[place + t] = value
            return inner

        return lax.fori_loop(block + 1, count, later, carry)

    lax.fori_loop(0, count, step, 0)


def solve(columns, cutting, factor):
    width, rows = columns.shape
    high = 8 if rows % 1024 == 0 else 1
    shape = (width, high, rows // high)
    out = pl.pallas_call(
        solve_kernel,
        out_shape=jax.ShapeDtypeStruct(shape, jnp.float32),
        in_specs=[
            pl.BlockSpec(memory_space=pltpu.SMEM),
            pl.BlockSpec(memory_space=pltpu.VMEM),
            pl.BlockSpec(memory_space=pltpu.VMEM),
        ],
        out_specs=pl.BlockSpec(memory_space=pltpu.VMEM),
        cost_estimate=pl.CostEstimate(
            flops=width * width * rows * 8, bytes_accessed=3 * width * rows * 4, transcendentals=0
        ),
    )(factor, columns.reshape(shape), cutting.reshape(shape))
    return out.reshape(width, rows)


def body(attn_out, residual, output_weight, prune_mask, inverse_factor, norm_gain, gate_up_weight):
    width_block = prune_mask.shape[1]
    tokens, width_part = attn_out.shape
    is_first = lax.axis_index("dp") == 0

    factor = from_first(inverse_factor[:, :width_block], "dp")
    columns = from_first(output_weight[:, :width_block], "dp")
    gain_rows = jnp.broadcast_to(norm_gain[None, :], (16, width_part))
    gathered = lax.all_gather(
        jnp.concatenate([attn_out, gain_rows], axis=0), "mp", axis=1, tiled=True
    )
    gain = gathered[tokens].astype(jnp.float32)
    features = exchange(gathered[:tokens], "dp")

    pivots = jnp.diagonal(factor)
    kept = prune_mask.astype(jnp.float32)
    cutting = ((1.0 - kept) / pivots[None, :]).T
    errors = solve(columns.astype(jnp.float32).T, cutting, factor)
    updated = output_weight.astype(jnp.float32) - lax.dot_general(
        errors, inverse_factor, (((0,), (0,)), ((), ())), preferred_element_type=jnp.float32
    )
    masking = jnp.where(is_first, kept, 1.0)
    masking = jnp.pad(
        masking, ((0, 0), (0, updated.shape[1] - width_block)), constant_values=1.0
    )
    pruned_weight = (updated * masking).astype(jnp.bfloat16)

    partial = lax.dot_general(
        features, pruned_weight, (((1,), (1,)), ((), ())), preferred_element_type=jnp.float32
    )
    projected = scatter_sum(partial, "dp")
    stream = (residual.astype(jnp.float32) + projected).astype(jnp.bfloat16)

    stream_all = lax.all_gather(stream, "mp", axis=1, tiled=True).astype(jnp.float32)
    squares = jnp.sum(stream_all * stream_all, axis=1, keepdims=True)
    inverse = lax.rsqrt(squares / stream_all.shape[1] + 1e-05)
    normed = (stream_all * inverse * gain[None, :]).astype(jnp.bfloat16)
    slices = exchange(normed, "dp")

    input_rows, _, unit_count = gate_up_weight.shape
    flat_weight = gate_up_weight.reshape(input_rows, 2 * unit_count)
    gate_up = scatter_sum(
        jnp.dot(slices, flat_weight, preferred_element_type=jnp.float32), "dp"
    )
    gate_part = gate_up[:, :unit_count]
    up_part = gate_up[:, unit_count:]
    hidden = (jax.nn.silu(gate_part) * up_part).astype(jnp.bfloat16)

    window_all = lax.all_gather(hidden, "dp", axis=0, tiled=True)
    columns_all = exchange(lax.all_gather(hidden, "mp", axis=1, tiled=True), "dp")
    weighting = 2.0 / (tokens * lax.axis_size("dp"))
    hessian = weighting * lax.dot_general(
        window_all, columns_all, (((0,), (0,)), ((), ())), preferred_element_type=jnp.float32
    )
    return (pruned_weight, stream, hessian)


def solution(mesh):
    in_specs = (
        P("dp", "mp"),
        P("dp", "mp"),
        P("mp", "dp"),
        P("mp", None),
        P(None, "dp"),
        P("mp"),
        P("dp", None, "mp"),
    )
    out_specs = (P("mp", "dp"), P("dp", "mp"), P("mp", "dp"))
    return jax.shard_map(body, mesh=mesh, in_specs=in_specs, out_specs=out_specs, check_vma=False)
```

time: 954 us -> 396 us (0.42)
  other arithmetic: 437 us -> 14 us
  waiting for transfers between devices: 372 us -> 242 us
  blocking collectives: 21.4 us -> 0 us
  matrix products: 54.6 us -> 36.3 us
  starting transfers between devices: 9.05 us -> 26.7 us
  Pallas kernels: 0 us -> 13.1 us
    another operation x12 -> x0, other arithmetic: 421 us -> none  [body(): jax.scipy.linalg.solve_triangular(system, target, lower=True, unit_diagon...]
    reduce_scatter x1 -> x0, waiting for transfers between devices: 63.7 us -> none  [body(): lax.psum_scatter(jnp.dot(slices, flat_weight, preferred_element_type=jnp....]
    all_gather x5 -> x4, waiting for transfers between devices: 219 us -> 178 us  [the longest x1 64.6 us: body(): lax.all_gather(hidden, 'mp', axis=1, tiled=True)]
    reshape x0 -> x6, local copies, waits for them, and re-layouts: none -> 40.2 us  [the longest x1 31 us: body(): flat_weight = gate_up_weight.reshape(input_rows, 2 * unit_count)]
    psum x1 -> x0, waiting for transfers between devices: 35.5 us -> none  [from_root(): return lax.psum(block, axis)]
    ppermute x0 -> x8, waiting for transfers between devices: none -> 33.3 us  [the longest x4 33.3 us: scatter_sum(): arrived = lax.ppermute(give.astype(jnp.bfloat16), axis, pairs)]
    unnamed x12 -> x6, local copies, waits for them, and re-layouts: 32 us -> 1.32 us
    all_to_all x2 -> x3, waiting for transfers between devices: 52.6 us -> 30.4 us  [exchange(): lax.all_to_all(blocks, axis, split_axis=0, concat_axis=0, tiled=True)]
  transfers between devices with their start and end apart: 9 -> 15, of which waited for: 8 -> 9; matrix products, arithmetic and copies ran while one was open for 4% -> 13% of each run, Pallas kernels for 0% -> 3%
where the time goes in v1:
time: 396 us; the launch traced here: 394 us
  waiting for transfers between devices  242 us (61%)
  local copies, waits for them, and re-layouts  47.9 us (12%)
  matrix products  36.3 us (9%)
  starting transfers between devices  26.7 us (7%)
  between operations  14.1 us (4%)
  other arithmetic  14 us (4%)
  Pallas kernels  13.1 us (3%)
    all_gather x1, waiting for transfers between devices, body(): lax.all_gather(hidden, 'mp', axis=1, tiled=True)  64.6 us
    all_gather x1, waiting for transfers between devices, body(): lax.all_gather(stream, 'mp', axis=1, tiled=True).astype(jnp.float32)  47.9 us
    all_gather x1, waiting for transfers between devices, body(): lax.all_gather(jnp.concatenate([attn_out, gain_rows], axis=0), 'mp', axis...  45.5 us
    ppermute x4, waiting for transfers between devices, scatter_sum(): arrived = lax.ppermute(give.astype(jnp.bfloat16), axis, pairs)  33.3 us
    reshape x1, local copies, waits for them, and re-layouts, body(): flat_weight = gate_up_weight.reshape(input_rows, 2 * unit_count)  31 us
    all_to_all x3, waiting for transfers between devices, exchange(): lax.all_to_all(blocks, axis, split_axis=0, concat_axis=0, tiled=True)  30.4 us
    all_gather x1, waiting for transfers between devices, body(): window_all = lax.all_gather(hidden, 'dp', axis=0, tiled=True)  19.7 us
    dot_general x1, matrix products, body(): lax.dot_general(window_all, columns_all, (((0,), (0,)), ((), ())), prefer...  14.7 us
  transfers between devices with their start and end apart: 15, of which 9 were waited for; matrix products, arithmetic and copies ran while one was open for 13% of the time, Pallas kernels for 3%

profile of v1, /device:TPU:0, one launch (start us, length us, event | category | flops | bytes accessed | tf_op | source)
XLA Modules:
  0.0 394.1 jit_solution(15240892957984006767)
XLA Ops:
  7.2 0.0 all-gather.5.cloned.1.call-start
  7.2 0.7 broadcast_in_dim.5
  7.9 1.7 pad_maximum_fusion
  9.6 0.0 all-gather.5.cloned.1.call-update
  9.6 0.8 slice.18
  10.5 4.9 %collective-permute-start = (f32[128,128]{1,0:T(8,128)S(1)}, f32[128,128]{1,0:T(8,128)S(1)}, u32[]{:S(2)}, u32[]{:S(2)}) collective-permute-start(f32[128,128]{1,0:T(8,128)S(1)} %slice.18), channel_id=1, source_target_pairs={{0,16},{1,17},{2,18},{3,19},{4,20},{5,21},{6,22},{7,23}} | collective-permute-start | bytes 196616 | tf_op jit(solution)/shard_map/ppermute | solution.py:18
  15.3 1.0 slice.19
  16.3 1.3 collective-permute-start.2
  17.6 0.9 broadcast_select_fusion.1
  18.5 1.3 collective-permute-start.1
  19.8 45.5 %all-gather.5.cloned.1.call-done = bf16[144,8192]{1,0:T(8,128)(2,1)} async-done(((bf16[144,1024]{1,0:T(8,128)(2,1)}), bf16[144,8192]{1,0:T(8,128)(2,1)}) %all-gather.5.cloned.1.call-update) | async-done | bytes 2359312 | tf_op jit(solution)/shard_map/all_gather | solution.py:107
  65.3 1.6 slice-done
  66.9 1.5 copy.41
  68.4 3.6 all-to-all-start
  72.0 0.0 all-gather.7.cloned.1.call-start
  72.1 0.0 collective-permute-done.1
  72.1 0.0 copy-start.1
  72.1 1.2 gather_fusion
  73.4 1.0 broadcast_select_fusion
  74.4 3.0 collective-permute-start.3
  77.4 1.1 subtract_divide_fusion
  78.5 1.0 copy.27.cutting_ref
  79.5 0.1 select_convert_fusion
  79.6 1.0 copy.26.weight_ref
  80.6 13.1 %shard_map.94 = f32[128,8,128]{2,1,0:T(8,128)} custom-call(f32[128,128]{1,0:T(8,128)} %copy-done.1, f32[128,8,128]{2,1,0:T(8,128)} %copy.26.weight_ref, f32[128,8,128]{2,1,0:T(8,128)} %copy.27.cutting_ref), custom_call_target="tpu_custom_call" | custom-call | flops 134217728 | bytes 1572864 | tf_op jit(solution)/shard_map/pallas_call | solution.py:83
  93.7 6.0 %multiply_convert_fusion = bf16[1024,2048]{1,0:T(8,128)(2,1)} fusion(f32[1024,128]{1,0:T(8,128)S(1)} %get-tuple-element.4, bf16[1024,2048]{1,0:T(8,128)(2,1)} %param.9, f32[128,2048]{1,0:T(8,128)} %param.11, f32[16,8,8,128]{3,2,1,0:T(8,128)} %bitcast.72), kind=kOutput, calls=%fused_computation.4 | convolution fusion | flops 545259520 | bytes 10485760 | tf_op jit(solution)/shard_map/dot_general | solution.py:117
  99.7 4.7 %fusion.5 = f32[2,2,128,1024]{3,2,1,0:T(8,128)S(1)} fusion(bf16[2,2,128,2048]{3,2,1,0:T(8,128)(2,1)S(1)} %bitcast.68, bf16[1024,2048]{1,0:T(8,128)(2,1)} %multiply_convert_fusion), kind=kOutput, calls=%fused_computation.10 | convolution fusion | flops 2147483648 | bytes 8388608 | tf_op jit(solution)/shard_map/dot_general | solution.py:126
  104.3 0.0 copy-start.2
  104.3 1.3 copy-done.2
  105.7 0.1 fusion.9
  105.7 0.1 collective-permute-start.4
  105.9 2.0 collective-permute-done.4
  107.8 1.5 bitcast_add_fusion.1
  109.4 0.7 dynamic-slice_convert_fusion.3
  110.1 1.6 collective-permute-start.5
  111.7 7.0 %collective-permute-done.5 = bf16[1,128,1024]{2,1,0:T(8,128)(2,1)} collective-permute-done((bf16[1,128,1024]{2,1,0:T(8,128)(2,1)}, bf16[1,128,1024]{2,1,0:T(8,128)(2,1)}, u32[]{:S(2)}, u32[]{:S(2)}) %collective-permute-start.5) | collective-permute-done | bytes 262176 | tf_op jit(solution)/shard_map/ppermute | solution.py:35
  118.8 1.8 fusion.12
  120.6 0.0 all-gather.7.cloned.1.call-update
  120.7 47.9 %all-gather.7.cloned.1.call-done = bf16[128,8192]{1,0:T(8,128)(2,1)} async-done(((bf16[128,1024]{1,0:T(8,128)(2,1)}), bf16[128,8192]{1,0:T(8,128)(2,1)}) %all-gather.7.cloned.1.call-update) | async-done | bytes 2097168 | tf_op jit(solution)/shard_map/all_gather | solution.py:132
  168.5 2.1 fusion.2
  170.6 2.2 fusion.4
  172.8 1.5 copy.40
  174.3 3.6 all-to-all-start.1
  177.9 0.2 all-gather.11.cloned.1.call-start
  178.1 31.0 %reshape.84 = bf16[2048,3584,1,1]{1,0,2,3:T(8,128)(2,1)} reshape(bf16[2048,2,1792]{2,1,0:T(2,128)(2,1)} %param.13) | data formatting | bytes 29360128 | tf_op jit(solution)/shard_map/reshape | solution.py:139
  209.2 11.0 %fusion = f32[2,2,128,3584]{3,2,1,0:T(8,128)S(1)} fusion(bf16[2,2,128,2048]{3,2,1,0:T(8,128)(2,1)S(1)} %bitcast.69, bf16[2048,3584,1,1]{1,0,2,3:T(8,128)(2,1)} %reshape.84), kind=kOutput, calls=%fused_computation.2 | convolution fusion | flops 7516192768 | bytes 24117248 | tf_op jit(solution)/shard_map/dot_general | solution.py:141
  220.2 0.2 fusion.7
  220.4 0.3 collective-permute-start.6
  220.7 3.6 collective-permute-done.6
  224.2 0.5 bitcast_add_fusion
  224.7 0.1 dynamic-slice_convert_fusion.1
  224.8 1.8 collective-permute-start.7
  226.6 20.7 %collective-permute-done.7 = bf16[1,128,3584]{2,1,0:T(8,128)(2,1)S(1)} collective-permute-done((bf16[1,128,3584]{2,1,0:T(8,128)(2,1)S(1)}, bf16[1,128,3584]{2,1,0:T(8,128)(2,1)S(1)}, u32[]{:S(2)}, u32[]{:S(2)}) %collective-permute-start.7) | collective-permute-done | bytes 917536 | tf_op jit(solution)/shard_map/ppermute | solution.py:35
  247.4 0.2 add_bitcast_fusion
  247.6 1.0 fusion.8
  248.6 0.0 all-gather.11.cloned.1.call-update
  248.6 0.0 all-gather.9.cloned.1.call-start
  248.7 0.5 all-gather.9.cloned.1.call-update
  249.2 64.6 %all-gather.11.cloned.1.call-done = bf16[128,14336]{1,0:T(8,128)(2,1)} async-done(((bf16[128,1792]{1,0:T(8,128)(2,1)}), bf16[128,14336]{1,0:T(8,128)(2,1)}) %all-gather.11.cloned.1.call-update) | async-done | bytes 3670032 | tf_op jit(solution)/shard_map/all_gather | solution.py:148
  313.8 4.2 %copy.39 = bf16[16,4,8,3584]{3,2,0,1:T(8,128)(2,1)} copy(bf16[16,4,8,3584]{3,2,1,0:T(8,128)(2,1)} %bitcast.67) | data formatting | bytes 7340032 | tf_op jit(solution)/shard_map/reshape | solution.py:45
  318.0 4.8 %all-to-all-start.2 = ((bf16[4,128,3584]{2,1,0:T(8,128)(2,1)}), bf16[4,128,3584]{2,1,0:T(8,128)(2,1)}, u32[]{:S(2)}, u32[]{:S(2)}) async-start(bf16[4,128,3584]{2,1,0:T(8,128)(2,1)} %bitcast.64), calls=%async_computation.2 | async-start | bytes 7340032 | tf_op jit(solution)/shard_map/all_to_all | solution.py:46
  322.8 19.7 %all-gather.9.cloned.1.call-done = bf16[512,1792]{1,0:T(8,128)(2,1)} async-done(((bf16[128,1792]{1,0:T(8,128)(2,1)}), bf16[512,1792]{1,0:T(8,128)(2,1)}) %all-gather.9.cloned.1.call-update) | async-done | bytes 1835024 | tf_op jit(solution)/shard_map/all_gather | solution.py:147
  342.6 30.3 %all-to-all-done.2 = bf16[4,128,3584]{2,1,0:T(8,128)(2,1)} async-done(((bf16[4,128,3584]{2,1,0:T(8,128)(2,1)}), bf16[4,128,3584]{2,1,0:T(8,128)(2,1)}, u32[]{:S(2)}, u32[]{:S(2)}) %all-to-all-start.2) | async-done | bytes 3670048 | tf_op jit(solution)/shard_map/all_to_all | solution.py:46
  372.9 14.7 %convolution_multiply_fusion = f32[1792,3584]{1,0:T(8,128)} fusion(bf16[512,1792]{1,0:T(8,128)(2,1)} %all-gather.9.cloned.1.call-done, bf16[512,3584]{1,0:T(8,128)(2,1)} %bitcast.20), kind=kOutput, calls=%fused_computation.1 | convolution fusion | flops 6583091200 | bytes 31195136 | tf_op jit(solution)/shard_map/dot_general | solution.py:150
  (13 shorter events, 0.1 us)
Async XLA Ops:
  7.2 58.1 %all-gather.5.cloned.1.call-start = ((), (), s32[]{:S(2)}) async-start(), calls=%async_computation.3 | async-start | bytes 2654208 | tf_op jit(solution)/shard_map/all_gather | solution.py:107
  10.5 7.2 %collective-permute-start = (f32[128,128]{1,0:T(8,128)S(1)}, f32[128,128]{1,0:T(8,128)S(1)}, u32[]{:S(2)}, u32[]{:S(2)}) collective-permute-start(f32[128,128]{1,0:T(8,128)S(1)} %slice.18), channel_id=1, source_target_pairs={{0,16},{1,17},{2,18},{3,19},{4,20},{5,21},{6,22},{7,23}} | collective-permute-start | bytes 196616 | tf_op jit(solution)/shard_map/ppermute | solution.py:18
  16.3 57.1 %collective-permute-start.2 = (bf16[1024,128]{1,0:T(8,128)(2,1)S(1)}, bf16[1024,128]{1,0:T(8,128)(2,1)S(1)}, u32[]{:S(2)}, u32[]{:S(2)}) collective-permute-start(bf16[1024,128]{1,0:T(8,128)(2,1)S(1)} %slice.19), channel_id=1, source_target_pairs={{0,16},{1,17},{2,18},{3,19},{4,20},{5,21},{6,22},{7,23}} | collective-permute-start | bytes 786440 | tf_op jit(solution)/shard_map/ppermute | solution.py:18
  18.5 53.6 %collective-permute-start.1 = (f32[128,128]{1,0:T(8,128)S(1)}, f32[128,128]{1,0:T(8,128)S(1)}, u32[]{:S(2)}, u32[]{:S(2)}) collective-permute-start(f32[128,128]{1,0:T(8,128)S(1)} %broadcast_select_fusion.1), channel_id=1, source_target_pairs={{0,8},{16,24},{1,9},{17,25},{2,10},{18,26},{3,11},{19,27},{4,12},{... | collective-permute-start | bytes 196616 | tf_op jit(solution)/shard_map/ppermute | solution.py:18
  65.3 1.6 slice-start
  68.4 31.3 %all-to-all-start = ((bf16[4,128,2048]{2,1,0:T(8,128)(2,1)}), bf16[4,128,2048]{2,1,0:T(8,128)(2,1)S(1)}, u32[]{:S(2)}, u32[]{:S(2)}) async-start(bf16[4,128,2048]{2,1,0:T(8,128)(2,1)} %bitcast.63), calls=%async_computation | async-start | bytes 4194304 | tf_op jit(solution)/shard_map/all_to_all | solution.py:46
  72.0 96.6 %all-gather.7.cloned.1.call-start = ((), (), s32[]{:S(2)}) async-start(), calls=%async_computation.4 | async-start | bytes 2359296 | tf_op jit(solution)/shard_map/all_gather | solution.py:132
  72.1 8.5 %copy-start.1 = (f32[128,128]{1,0:T(8,128)}, f32[128,128]{1,0:T(8,128)S(1)}, u32[]{:S(2)}) copy-start(f32[128,128]{1,0:T(8,128)S(1)} %broadcast_select_fusion.2.factor_ref) | copy-start | bytes 196612
  74.4 5.2 %collective-permute-start.3 = (bf16[1024,128]{1,0:T(8,128)(2,1)S(1)}, bf16[1024,128]{1,0:T(8,128)(2,1)}, u32[]{:S(2)}, u32[]{:S(2)}) collective-permute-start(bf16[1024,128]{1,0:T(8,128)(2,1)S(1)} %broadcast_select_fusion), channel_id=1, source_target_pairs={{0,8},{16,24},{1,9},{17,25},{2,10},{18,26},{3,11},{19,27},{4,12},{... | collective-permute-start | bytes 786440 | tf_op jit(solution)/shard_map/ppermute | solution.py:18
  104.3 1.3 copy-start.2
  105.7 15.0 %copy-start = (bf16[144,8192]{1,0:T(8,128)(2,1)S(1)}, bf16[144,8192]{1,0:T(8,128)(2,1)}, u32[]{:S(2)}) copy-start(bf16[144,8192]{1,0:T(8,128)(2,1)} %all-gather.5.cloned.1.call-done) | copy-start | bytes 7077892
  105.7 2.1 collective-permute-start.4
  110.1 8.7 %collective-permute-start.5 = (bf16[1,128,1024]{2,1,0:T(8,128)(2,1)}, bf16[1,128,1024]{2,1,0:T(8,128)(2,1)}, u32[]{:S(2)}, u32[]{:S(2)}) collective-permute-start(bf16[1,128,1024]{2,1,0:T(8,128)(2,1)} %dynamic-slice_convert_fusion.3), channel_id=1, source_target_pairs={{0,16},{8,24},{16,0},{24,8},{1,17},{9,25},{17,1},{25,9},{2,18},{10... | collective-permute-start | bytes 786440 | tf_op jit(solution)/shard_map/ppermute | solution.py:35
  174.3 34.9 %all-to-all-start.1 = ((bf16[4,128,2048]{2,1,0:T(8,128)(2,1)}), bf16[4,128,2048]{2,1,0:T(8,128)(2,1)S(1)}, u32[]{:S(2)}, u32[]{:S(2)}) async-start(bf16[4,128,2048]{2,1,0:T(8,128)(2,1)} %bitcast.61), calls=%async_computation.1 | async-start | bytes 4194304 | tf_op jit(solution)/shard_map/all_to_all | solution.py:46
  177.9 135.9 %all-gather.11.cloned.1.call-start = ((), (), s32[]{:S(2)}) async-start(), calls=%async_computation.6 | async-start | bytes 4128768 | tf_op jit(solution)/shard_map/all_gather | solution.py:148
  220.4 3.9 collective-permute-start.6
  224.8 22.6 %collective-permute-start.7 = (bf16[1,128,3584]{2,1,0:T(8,128)(2,1)S(1)}, bf16[1,128,3584]{2,1,0:T(8,128)(2,1)S(1)}, u32[]{:S(2)}, u32[]{:S(2)}) collective-permute-start(bf16[1,128,3584]{2,1,0:T(8,128)(2,1)S(1)} %dynamic-slice_convert_fusion.1), channel_id=1, source_target_pairs={{0,16},{8,24},{16,0},{24,8},{1,17},{9,25},{17,1},{25,9},{2,18},{10... | collective-permute-start | bytes 2752520 | tf_op jit(solution)/shard_map/ppermute | solution.py:35
  248.6 93.9 %all-gather.9.cloned.1.call-start = ((), (), s32[]{:S(2)}) async-start(), calls=%async_computation.5 | async-start | bytes 2293760 | tf_op jit(solution)/shard_map/all_gather | solution.py:147
  318.0 54.9 %all-to-all-start.2 = ((bf16[4,128,3584]{2,1,0:T(8,128)(2,1)}), bf16[4,128,3584]{2,1,0:T(8,128)(2,1)}, u32[]{:S(2)}, u32[]{:S(2)}) async-start(bf16[4,128,3584]{2,1,0:T(8,128)(2,1)} %bitcast.64), calls=%async_computation.2 | async-start | bytes 7340032 | tf_op jit(solution)/shard_map/all_to_all | solution.py:46
Sparse Core Ops, SparseCore 0:
  10.7 54.5 all-gather.4
  120.7 47.7 all-gather.6
  248.7 64.9 all-gather.10
  315.2 27.3 all-gather.8
